TPU v7x, 32 devices: a whole 2x2x4 slice. The times are simulated.
32 devices in a mesh: dp: 16 (over z, y, core), tensor: 2 (over x).
Axes of the slice: x: 2, y: 2, z: 4, core: 2. Of those that a mesh axis runs over, the one named last changes fastest.
Arguments:
- attn_out: bfloat16 [12288, 2048], P('dp', 'tensor'), may hold values from -6 to 6
- out_proj_t: bfloat16 [4096, 2048], P(None, 'tensor'), may hold values from -0.09375 to 0.09375
- grad_out: bfloat16 [12288, 4096], P('dp', 'tensor'), may hold values from -6 to 6
- read_weights: float32 [12288, 16], P('dp'), may hold values from 0 to 0.0026041667
- memory_gate: float32 [256, 16], P('dp'), may hold values from -0.2 to 1
- write_pos: int32 [16, 16], P('dp'), may hold values from 0 to 767, as said below
Outputs:
- grad_attn_out: bfloat16 [12288, 2048], P('dp', 'tensor')
- grad_out_proj_t: float32 [4096, 2048], P('dp', 'tensor')
- grad_memory: float32 [256, 4096], P('dp', 'tensor')
Inputs may be any that keep to these rules, and one draw needn't show every extreme that they name: `write_pos`: the 16 positions of one segment are distinct.
All inputs are finite; a program needn't handle non-finite values.
Results may differ from a plain program's by a relative error of at most 0.0034.
Values may be sent and summed in bfloat16 or wider, within the bound.
No kernel may reach another device: no remote copies, remote signals or barrier semaphores. Data moves between devices by JAX's collectives and lax.ppermute only.
A program may use at most 64 MiB of HBM per device.

v0:
```python
import jax
import jax.numpy as jnp
from jax import lax
from jax.sharding import PartitionSpec as P

F32 = jnp.float32
BF16 = jnp.bfloat16


def grid_of(count):
    cores = 2 if count % 2 == 0 else 1
    chips = count // cores
    rows = 1
    while chips % (rows * 2) == 0 and (rows * 2) ** 2 <= chips:
        rows *= 2
    return chips // rows, rows, cores


def cuts_of(rows):
    if rows % 128 or rows == 128:
        return [(0, rows)]
    return [(0, rows // 2), (rows // 2, rows)]


def body(attn_out, out_proj_t, grad_out, read_weights, memory_gate, write_pos):
    high = lax.Precision.HIGHEST
    seg_len, own_width = grad_out.shape
    heads = attn_out.shape[1]
    slots = write_pos.shape[1]
    count = lax.axis_size("dp")
    parts = lax.axis_size("tensor")
    mine = lax.axis_index("dp")
    side = lax.axis_index("tensor")
    deep, wide, cores = grid_of(count)
    rows = own_width * parts // count
    held = own_width // rows
    pairs = held // cores
    place = (mine // (wide * cores), (mine // cores) % wide, mine % cores)

    def shift_tensor(x, r):
        return lax.ppermute(x, "tensor", [(t, (t + r) % parts) for t in range(parts)])

    def shift_dp(x, axis, move):
        moves = []
        for i in range(count):
            at = [i // (wide * cores), (i // cores) % wide, i % cores]
            at[axis] = move(at[axis])
            moves.append((i, (at[0] * wide + at[1]) * cores + at[2]))
        return lax.ppermute(x, "dp", moves)

    cuts = cuts_of(rows)

    def columns(x, lo, hi):
        return jnp.concatenate(
            [
                x[:, (p * cores + c) * rows + lo : (p * cores + c) * rows + hi]
                for c in range(cores)
                for p in range(pairs)
            ],
            axis=1,
        )

    own = [columns(grad_out, lo, hi) for lo, hi in cuts]
    got = [[shift_tensor(own[0], r) for r in range(1, parts)]]

    top = lax.reduce_precision(read_weights, 8, 7)
    rest = read_weights - top
    mid = lax.reduce_precision(rest, 8, 7)
    low = rest - mid
    terms = jnp.concatenate([top, mid, low], axis=1).astype(BF16)
    local3 = lax.dot_general(terms, grad_out, (((0,), (0,)), ((), ())), preferred_element_type=F32)
    local = local3[:slots] + local3[slots : 2 * slots] + local3[2 * slots :]

    gate = memory_gate.T
    lanes = 128 * (-(-slots // 128))
    maps = jnp.concatenate([local, jnp.pad(gate, ((0, 0), (0, lanes - slots)))], axis=1)
    base = jnp.pad(local, ((0, 0), (0, lanes)))

    def later(x, r):
        return lax.ppermute(x, "dp", [(i, i - r) for i in range(r, count)])

    step = 1
    acc = maps
    while step < count:
        come = later(acc, step)
        head = acc[:, own_width : own_width + slots]
        keep = jnp.pad(acc[:, :own_width], ((0, 0), (0, lanes)))
        acc = keep + jnp.dot(head, come, precision=high, preferred_element_type=F32)
        step *= 2
    grad_memory = acc[:, :own_width]
    after = later(grad_memory, 1)

    places = jnp.arange(seg_len, dtype=jnp.int32)
    hits = places[:, None] == write_pos[0][None, :]
    onehot = hits.astype(BF16)
    touched = jnp.any(hits, axis=1)[:, None]
    picked = lax.dot_general(onehot, grad_out, (((0,), (0,)), ((), ())), preferred_element_type=F32)
    fresh = (picked + after).astype(BF16)
    fresh_got = [shift_tensor(fresh, r) for r in range(1, parts)]
    for k in range(1, len(cuts)):
        got.append([shift_tensor(own[k], r) for r in range(1, parts)])

    def ordered(pieces):
        out = []
        for q in range(parts):
            pick = pieces[0]
            for r in range(1, parts):
                pick = jnp.where((side - r) % parts == q, pieces[r], pick)
            out.append(pick)
        return out

    def put_rows(dy_cut, row_cut):
        put = jnp.dot(onehot, row_cut, preferred_element_type=F32).astype(BF16)
        return jnp.where(touched, put, dy_cut)

    def near_sum(z_cut, size):
        width = pairs * size

        def of_core(c):
            lhs = lax.dynamic_slice_in_dim(z_cut, c * width, width, 1)
            return lax.dot_general(
                lhs, attn_out, (((0,), (0,)), ((), ())), preferred_element_type=F32
            )

        if cores == 2:
            away = of_core(1 - place[2]).astype(BF16)
            part = of_core(place[2])
            part = part + shift_dp(away, 2, lambda v: 1 - v).astype(F32)
        else:
            part = of_core(0)
        part = part.reshape(pairs // wide, wide, size, heads)
        here = place[1]
        total = lax.dynamic_index_in_dim(part, here, 1, keepdims=False)
        for r in range(1, wide):
            there = lax.dynamic_index_in_dim(part, (here + r) % wide, 1, keepdims=False)
            come = shift_dp(there.astype(BF16), 1, lambda v: (v + r) % wide)
            total = total + come.astype(F32)
        return total

    def deep_sum(x):
        bit = 1
        while bit < deep:
            x = x.reshape((x.shape[0] // 2, 2) + x.shape[1:])
            here = (place[0] // bit) % 2
            away = lax.dynamic_index_in_dim(x, 1 - here, 1, keepdims=False).astype(BF16)
            come = shift_dp(away, 0, lambda v: v ^ bit)
            x = lax.dynamic_index_in_dim(x, here, 1, keepdims=False) + come.astype(F32)
            bit *= 2
        return x[0]

    proj = out_proj_t.reshape(parts, pairs, cores, rows, heads)
    z_own, near_own, row_cuts = [], [], []
    for k, (lo, hi) in enumerate(cuts):
        row_cuts.append([columns(x, lo, hi) for x in [fresh] + fresh_got])
        z_own.append(put_rows(own[k], row_cuts[k][0]))
        near_own.append(near_sum(z_own[k], hi - lo))
    grad_attn = None
    sums = []
    for k, (lo, hi) in enumerate(cuts):
        z_got = [put_rows(x, y) for x, y in zip(got[k], row_cuts[k][1:])]
        near = [near_own[k]] + [near_sum(z, hi - lo) for z in z_got]
        sums.append(deep_sum(jnp.concatenate(ordered(near), axis=0)))
        w_cut = proj[:, :, :, lo:hi].transpose(0, 2, 1, 3, 4).reshape(parts, -1, heads)
        for r, z in enumerate([z_own[k]] + z_got):
            w = lax.dynamic_index_in_dim(w_cut, (side - r) % parts, 0, keepdims=False)
            term = jnp.dot(z, w, preferred_element_type=F32)
            grad_attn = term if grad_attn is None else grad_attn + term
    grad_weight = jnp.concatenate(sums, axis=0)
    return (grad_attn.astype(BF16), grad_weight, grad_memory)


def solution(mesh):
    return jax.shard_map(
        body,
        mesh=mesh,
        in_specs=(
            P("dp", "tensor"),
            P(None, "tensor"),
            P("dp", "tensor"),
            P("dp", None),
            P("dp", None),
            P("dp", None),
        ),
        out_specs=(P("dp", "tensor"), P("dp", "tensor"), P("dp", "tensor")),
        check_vma=False,
    )
```

profile of v0, /device:TPU:0, one launch (start us, length us, event | category | flops | bytes accessed | tf_op | source)
XLA Modules:
  0.0 187.6 jit_solution(17359403508261156536)
XLA Ops:
  0.6 0.9 copy.27
  1.5 0.8 reduce-precision_convert_fusion.1
  2.4 2.7 %fusion.39 = f32[48,2048]{1,0:T(8,128)S(1)} fusion(bf16[768,2048]{1,0:T(8,128)(2,1)} %param.8, bf16[768,16]{0,1:T(8,128)(2,1)S(1)} %get-tuple-element.54, bf16[768,16]{0,1:T(8,128)(2,1)S(1)} %get-tuple-element.55, bf16[768,16]{0,1:T(8,128)(2,1)S(1)} %get-tuple-element.53), kind=kOutput, calls=%fused_computation.129 | convolution fusion | flops 151216128 | bytes 3612672 | tf_op jit(solution)/shard_map/dot_general | solution.py:71
  5.2 1.6 collective-permute-start
  8.2 0.7 slice_dynamic-update-slice_fusion.13
  12.9 1.3 collective-permute-start.1
  14.3 8.5 %collective-permute-done.1 = f32[16,2176]{1,0:T(8,128)S(1)} collective-permute-done((f32[16,2176]{1,0:T(8,128)S(1)}, f32[16,2176]{1,0:T(8,128)S(1)}, u32[]{:S(2)}, u32[]{:S(2)}) %collective-permute-start.1) | collective-permute-done | bytes 139296 | tf_op jit(solution)/shard_map/ppermute | solution.py:80
  23.1 1.3 collective-permute-start.2
  24.5 1.7 collective-permute-start.7
  26.5 3.9 %collective-permute-done.2 = f32[16,2176]{1,0:T(8,128)S(1)} collective-permute-done((f32[16,2176]{1,0:T(8,128)S(1)}, f32[16,2176]{1,0:T(8,128)S(1)}, u32[]{:S(2)}, u32[]{:S(2)}) %collective-permute-start.2) | collective-permute-done | bytes 139296 | tf_op jit(solution)/shard_map/ppermute | solution.py:80
  30.7 1.3 collective-permute-start.3
  32.0 3.8 %slice_bitcast_fusion.1 = (bf16[2,2,4,128,1024]{4,3,1,2,0:T(8,128)(2,1)}, bf16[2,2,4,128,1024]{4,3,1,2,0:T(8,128)(2,1)}) fusion(bf16[2,4,2,256,1024]{4,3,2,1,0:T(8,128)(2,1)S(1)} %bitcast.120), kind=kLoop, calls=%fused_computation.1 | loop fusion | bytes 16777216 | tf_op jit(solution)/shard_map/transpose | solution.py:163
  35.9 4.6 %collective-permute-done.3 = f32[16,2176]{1,0:T(8,128)S(1)} collective-permute-done((f32[16,2176]{1,0:T(8,128)S(1)}, f32[16,2176]{1,0:T(8,128)S(1)}, u32[]{:S(2)}, u32[]{:S(2)}) %collective-permute-start.3) | collective-permute-done | bytes 139296 | tf_op jit(solution)/shard_map/ppermute | solution.py:80
  40.8 1.5 collective-permute-start.4
  43.0 4.9 %copy.28 = bf16[2,2,4,128,1024]{4,3,2,1,0:T(8,128)(2,1)} copy(bf16[2,2,4,128,1024]{4,3,1,2,0:T(8,128)(2,1)} %get-tuple-element.3) | data formatting | bytes 8388608 | tf_op jit(solution)/shard_map/transpose | solution.py:163
  47.9 2.4 %copy.29 = bf16[2,2,4,128,1024]{4,3,2,1,0:T(8,128)(2,1)} copy(bf16[2,2,4,128,1024]{4,3,1,2,0:T(8,128)(2,1)S(1)} %copy-done.2) | data formatting | bytes 8388608 | tf_op jit(solution)/shard_map/transpose | solution.py:163
  50.5 1.7 collective-permute-start.5
  53.0 1.0 convolution_convert_fusion.4
  54.0 0.9 collective-permute-start.16
  54.9 2.1 %broadcast_select_fusion.3 = bf16[768,1024]{1,0:T(8,128)(2,1)S(1)} fusion(bf16[768,1024]{1,0:T(8,128)(2,1)} %get-tuple-element.9, pred[768]{0:T(1024)(128)(4,1)S(1)} %fusion.47, bf16[16,1024]{1,0:T(8,128)(2,1)S(1)} %get-tuple-element.37, s32[16]{0:T(128)S(1)} %bitcast.141), kind=kOutput, calls=%fused_computation.30 | convolution fusion | flops 26750976 | bytes 3179328 | tf_op jit(solution)/shard_map/dot_general | solution.py:113
  57.0 1.0 convolution_convert_fusion.6
  58.2 1.0 copy-done.5
  59.2 1.8 fusion.7
  61.4 1.8 fusion.3
  63.2 32.8 %collective-permute-done.5 = bf16[16,2048]{1,0:T(8,128)(2,1)S(1)} collective-permute-done((bf16[16,2048]{1,0:T(8,128)(2,1)S(1)}, bf16[16,2048]{1,0:T(8,128)(2,1)S(1)}, u32[]{:S(2)}, u32[]{:S(2)}) %collective-permute-start.5) | collective-permute-done | bytes 65568 | tf_op jit(solution)/shard_map/ppermute | solution.py:41
  96.1 2.1 %broadcast_select_fusion = bf16[768,1024]{1,0:T(8,128)(2,1)S(1)} fusion(bf16[768,1024]{1,0:T(8,128)(2,1)} %collective-permute-done.7, pred[768]{0:T(1024)(128)(4,1)S(1)} %fusion.47, bf16[16,1024]{1,0:T(8,128)(2,1)S(1)} %get-tuple-element.21, s32[16]{0:T(128)S(1)} %bitcast.142), kind=kOutput, calls=%fused_computation.27 | convolution fusion | flops 26750976 | bytes 3179328 | tf_op jit(solution)/shard_map/dot_general | solution.py:113
  98.2 1.0 convolution_convert_fusion.5
  99.3 2.1 %broadcast_select_fusion.2 = bf16[768,1024]{1,0:T(8,128)(2,1)S(1)} fusion(bf16[768,1024]{1,0:T(8,128)(2,1)} %collective-permute-done.6, pred[768]{0:T(1024)(128)(4,1)S(1)} %fusion.47, bf16[16,1024]{1,0:T(8,128)(2,1)S(1)} %get-tuple-element.22, s32[16]{0:T(128)S(1)} %bitcast.143), kind=kOutput, calls=%fused_computation.29 | convolution fusion | flops 26750976 | bytes 3179328 | tf_op jit(solution)/shard_map/dot_general | solution.py:113
  101.4 1.0 convolution_convert_fusion.7
  103.0 1.0 convert_add_fusion
  104.1 2.3 %collective-permute-start.17 = (bf16[2,128,1024]{2,1,0:T(8,128)(2,1)S(1)}, bf16[2,128,1024]{2,1,0:T(8,128)(2,1)S(1)}, u32[]{:S(2)}, u32[]{:S(2)}) collective-permute-start(bf16[2,128,1024]{2,1,0:T(8,128)(2,1)S(1)} %fusion.35), channel_id=1, source_target_pairs={{0,4},{2,6},{4,0},{6,2},{8,12},{10,14},{12,8},{14,10},{16,20},{18,... | collective-permute-start | bytes 1572872 | tf_op jit(solution)/shard_map/ppermute | solution.py:49
  106.4 1.0 convert_add_fusion.2
  107.4 1.3 convert_add_fusion.1
  109.0 2.1 %collective-permute-start.11 = (bf16[2,128,1024]{2,1,0:T(8,128)(2,1)S(1)}, bf16[2,128,1024]{2,1,0:T(8,128)(2,1)S(1)}, u32[]{:S(2)}, u32[]{:S(2)}) collective-permute-start(bf16[2,128,1024]{2,1,0:T(8,128)(2,1)S(1)} %fusion.37), channel_id=1, source_target_pairs={{0,4},{2,6},{4,0},{6,2},{8,12},{10,14},{12,8},{14,10},{16,20},{18,... | collective-permute-start | bytes 1572872 | tf_op jit(solution)/shard_map/ppermute | solution.py:49
  111.0 1.0 convert_add_fusion.3
  112.2 6.9 %collective-permute-done.17 = bf16[2,128,1024]{2,1,0:T(8,128)(2,1)S(1)} collective-permute-done((bf16[2,128,1024]{2,1,0:T(8,128)(2,1)S(1)}, bf16[2,128,1024]{2,1,0:T(8,128)(2,1)S(1)}, u32[]{:S(2)}, u32[]{:S(2)}) %collective-permute-start.17) | collective-permute-done | bytes 524320 | tf_op jit(solution)/shard_map/ppermute | solution.py:49
  119.2 11.2 %collective-permute-done.15 = bf16[2,128,1024]{2,1,0:T(8,128)(2,1)S(1)} collective-permute-done((bf16[2,128,1024]{2,1,0:T(8,128)(2,1)S(1)}, bf16[2,128,1024]{2,1,0:T(8,128)(2,1)S(1)}, u32[]{:S(2)}, u32[]{:S(2)}) %collective-permute-start.15) | collective-permute-done | bytes 524320 | tf_op jit(solution)/shard_map/ppermute | solution.py:49
  131.1 2.4 %collective-permute-start.18 = (bf16[2,128,1024]{2,1,0:T(8,128)(2,1)S(1)}, bf16[2,128,1024]{2,1,0:T(8,128)(2,1)S(1)}, u32[]{:S(2)}, u32[]{:S(2)}) collective-permute-start(bf16[2,128,1024]{2,1,0:T(8,128)(2,1)S(1)} %fusion.38), channel_id=1, source_target_pairs={{0,8},{2,10},{4,12},{6,14},{8,0},{10,2},{12,4},{14,6},{16,24},{18,... | collective-permute-start | bytes 1572872 | tf_op jit(solution)/shard_map/ppermute | solution.py:49
  133.6 8.1 %collective-permute-done.11 = bf16[2,128,1024]{2,1,0:T(8,128)(2,1)S(1)} collective-permute-done((bf16[2,128,1024]{2,1,0:T(8,128)(2,1)S(1)}, bf16[2,128,1024]{2,1,0:T(8,128)(2,1)S(1)}, u32[]{:S(2)}, u32[]{:S(2)}) %collective-permute-start.11) | collective-permute-done | bytes 524320 | tf_op jit(solution)/shard_map/ppermute | solution.py:49
  141.7 10.6 %collective-permute-done.9 = bf16[2,128,1024]{2,1,0:T(8,128)(2,1)S(1)} collective-permute-done((bf16[2,128,1024]{2,1,0:T(8,128)(2,1)S(1)}, bf16[2,128,1024]{2,1,0:T(8,128)(2,1)S(1)}, u32[]{:S(2)}, u32[]{:S(2)}) %collective-permute-start.9) | collective-permute-done | bytes 524320 | tf_op jit(solution)/shard_map/ppermute | solution.py:49
  152.9 2.4 %collective-permute-start.12 = (bf16[2,128,1024]{2,1,0:T(8,128)(2,1)S(1)}, bf16[2,128,1024]{2,1,0:T(8,128)(2,1)S(1)}, u32[]{:S(2)}, u32[]{:S(2)}) collective-permute-start(bf16[2,128,1024]{2,1,0:T(8,128)(2,1)S(1)} %fusion.33), channel_id=1, source_target_pairs={{0,8},{2,10},{4,12},{6,14},{8,0},{10,2},{12,4},{14,6},{16,24},{18,... | collective-permute-start | bytes 1572872 | tf_op jit(solution)/shard_map/ppermute | solution.py:49
  155.4 1.8 fusion.5
  157.4 2.7 %collective-permute-start.19 = (bf16[1,128,1024]{2,1,0:T(8,128)(2,1)S(1)}, bf16[1,128,1024]{2,1,0:T(8,128)(2,1)S(1)}, u32[]{:S(2)}, u32[]{:S(2)}) collective-permute-start(bf16[1,128,1024]{2,1,0:T(8,128)(2,1)S(1)} %dynamic-slice_convert_fusion.1), channel_id=1, source_target_pairs={{0,16},{2,18},{4,20},{6,22},{8,24},{10,26},{12,28},{14,30},{16,0},... | collective-permute-start | bytes 786440 | tf_op jit(solution)/shard_map/ppermute | solution.py:49
  160.0 12.5 %collective-permute-done.12 = bf16[2,128,1024]{2,1,0:T(8,128)(2,1)S(1)} collective-permute-done((bf16[2,128,1024]{2,1,0:T(8,128)(2,1)S(1)}, bf16[2,128,1024]{2,1,0:T(8,128)(2,1)S(1)}, u32[]{:S(2)}, u32[]{:S(2)}) %collective-permute-start.12) | collective-permute-done | bytes 524320 | tf_op jit(solution)/shard_map/ppermute | solution.py:49
  172.7 1.9 %collective-permute-start.13 = (bf16[1,128,1024]{2,1,0:T(8,128)(2,1)S(1)}, bf16[1,128,1024]{2,1,0:T(8,128)(2,1)S(1)}, u32[]{:S(2)}, u32[]{:S(2)}) collective-permute-start(bf16[1,128,1024]{2,1,0:T(8,128)(2,1)S(1)} %dynamic-slice_convert_fusion.2), channel_id=1, source_target_pairs={{0,16},{2,18},{4,20},{6,22},{8,24},{10,26},{12,28},{14,30},{16,0},... | collective-permute-start | bytes 786440 | tf_op jit(solution)/shard_map/ppermute | solution.py:49
  174.7 3.0 %add_convert_fusion = bf16[768,1024]{1,0:T(8,128)(2,1)} fusion(f32[768,1024]{1,0:T(8,128)S(1)} %fusion.3, f32[768,1024]{1,0:T(8,128)S(1)} %fusion.7, f32[768,1024]{1,0:T(8,128)S(1)} %fusion.5, bf16[768,1024]{1,0:T(8,128)(2,1)S(1)} %broadcast_select_fusion, bf16[2,1024,1024]{2,1,0:T(8,128)(2,1)S(1)} %bitcast.126, s32[]{:T(128)S(6)} %select_n.157), kind=kOutput, calls=%fused_computation.4 | convolution fusion | flops 1613758464 | bytes 14680068 | tf_op jit(solution)/shard_map/dot_general | solution.py:166
  177.7 8.7 %collective-permute-done.13 = bf16[1,128,1024]{2,1,0:T(8,128)(2,1)S(1)} collective-permute-done((bf16[1,128,1024]{2,1,0:T(8,128)(2,1)S(1)}, bf16[1,128,1024]{2,1,0:T(8,128)(2,1)S(1)}, u32[]{:S(2)}, u32[]{:S(2)}) %collective-permute-start.13) | collective-permute-done | bytes 262176 | tf_op jit(solution)/shard_map/ppermute | solution.py:49
  186.5 1.0 pad_maximum_fusion.2
  (89 shorter events, 11.7 us)
Async XLA Ops:
  0.6 52.3 %copy-start = (bf16[768,1024]{1,0:T(8,128)(2,1)S(1)}, bf16[768,1024]{1,0:T(8,128)(2,1)}, u32[]{:S(2)}) copy-start(bf16[768,1024]{1,0:T(8,128)(2,1)} %param.6) | copy-start | bytes 4718596
  1.5 11.1 %copy-start.7 = (f32[16,16]{1,0:T(8,128)S(1)}, f32[16,16]{1,0:T(8,128)}, u32[]{:S(2)}) copy-start(f32[16,16]{1,0:T(8,128)} %param.10) | copy-start | bytes 3076
  1.5 21.3 %copy-start.8 = (pred[2176]{0:T(1024)(128)(4,1)S(1)}, pred[2176]{0:T(1024)(128)(4,1)}, u32[]{:S(2)}) copy-start(pred[2176]{0:T(1024)(128)(4,1)} %constant.159.clone.1) | copy-start | bytes 6532
  2.4 4.3 %copy-start.1 = (bf16[768,2048]{1,0:T(8,128)(2,1)S(1)}, bf16[768,2048]{1,0:T(8,128)(2,1)}, u32[]{:S(2)}) copy-start(bf16[768,2048]{1,0:T(8,128)(2,1)} %param.8) | copy-start | bytes 9437188
  2.4 29.6 %copy-start.3 = (bf16[4096,1024]{1,0:T(8,128)(2,1)S(1)}, bf16[4096,1024]{1,0:T(8,128)(2,1)}, u32[]{:S(2)}) copy-start(bf16[4096,1024]{1,0:T(8,128)(2,1)} %param.7) | copy-start | bytes 25165828
  5.2 7.4 %collective-permute-start = (f32[16,2176]{1,0:T(8,128)S(1)}, f32[16,2176]{1,0:T(8,128)S(1)}, u32[]{:S(2)}, u32[]{:S(2)}) collective-permute-start(f32[16,2176]{1,0:T(8,128)S(1)} %select_maximum_fusion), channel_id=1, source_target_pairs={{2,0},{4,2},{6,4},{8,6},{10,8},{12,10},{14,12},{16,14},{18,16},{20... | collective-permute-start | bytes 417800 | tf_op jit(solution)/shard_map/ppermute | solution.py:80
  12.9 9.9 %collective-permute-start.1 = (f32[16,2176]{1,0:T(8,128)S(1)}, f32[16,2176]{1,0:T(8,128)S(1)}, u32[]{:S(2)}, u32[]{:S(2)}) collective-permute-start(f32[16,2176]{1,0:T(8,128)S(1)} %fusion), channel_id=1, source_target_pairs={{4,0},{6,2},{8,4},{10,6},{12,8},{14,10},{16,12},{18,14},{20,16},{2... | collective-permute-start | bytes 417800 | tf_op jit(solution)/shard_map/ppermute | solution.py:80
  23.1 7.4 %collective-permute-start.2 = (f32[16,2176]{1,0:T(8,128)S(1)}, f32[16,2176]{1,0:T(8,128)S(1)}, u32[]{:S(2)}, u32[]{:S(2)}) collective-permute-start(f32[16,2176]{1,0:T(8,128)S(1)} %select_add_fusion.1), channel_id=1, source_target_pairs={{8,0},{10,2},{12,4},{14,6},{16,8},{18,10},{20,12},{22,14},{24,16},... | collective-permute-start | bytes 417800 | tf_op jit(solution)/shard_map/ppermute | solution.py:80
  24.5 71.6 %collective-permute-start.7 = (bf16[768,1024]{1,0:T(8,128)(2,1)S(1)}, bf16[768,1024]{1,0:T(8,128)(2,1)}, u32[]{:S(2)}, u32[]{:S(2)}) collective-permute-start(bf16[768,1024]{1,0:T(8,128)(2,1)S(1)} %slice_dynamic-update-slice_fusion), channel_id=1, source_target_pairs={{0,1},{1,0},{2,3},{3,2},{4,5},{5,4},{6,7},{7,6},{8,9},{9,8},{10,11... | collective-permute-start | bytes 4718600 | tf_op jit(solution)/shard_map/ppermute | solution.py:41
  26.2 73.1 %collective-permute-start.6 = (bf16[768,1024]{1,0:T(8,128)(2,1)}, bf16[768,1024]{1,0:T(8,128)(2,1)}, u32[]{:S(2)}, u32[]{:S(2)}) collective-permute-start(bf16[768,1024]{1,0:T(8,128)(2,1)} %get-tuple-element.9), channel_id=1, source_target_pairs={{0,1},{1,0},{2,3},{3,2},{4,5},{5,4},{6,7},{7,6},{8,9},{9,8},{10,11... | collective-permute-start | bytes 4718600 | tf_op jit(solution)/shard_map/ppermute | solution.py:41
  30.7 9.8 %collective-permute-start.3 = (f32[16,2176]{1,0:T(8,128)S(1)}, f32[16,2176]{1,0:T(8,128)S(1)}, u32[]{:S(2)}, u32[]{:S(2)}) collective-permute-start(f32[16,2176]{1,0:T(8,128)S(1)} %select_add_fusion), channel_id=1, source_target_pairs={{16,0},{18,2},{20,4},{22,6},{24,8},{26,10},{28,12},{30,14},{17,1},... | collective-permute-start | bytes 417800 | tf_op jit(solution)/shard_map/ppermute | solution.py:80
  32.0 8.7 %slice-start = ((pred[2176]{0:T(1024)(128)(4,1)}), pred[2048]{0:T(1024)(128)(4,1)S(1)}, s32[]{:S(2)}) async-start(pred[2176]{0:T(1024)(128)(4,1)} %constant.159.clone.1), calls=%async_computation | async-start | bytes 4096 | tf_op jit(solution)/shard_map/slice | solution.py:90
  32.0 10.3 %copy-start.9 = (s32[1,16]{1,0:T(1,128)S(1)}, s32[1,16]{1,0:T(1,128)}, u32[]{:S(2)}) copy-start(s32[1,16]{1,0:T(1,128)} %param.11) | copy-start | bytes 196
  40.8 2.1 %copy-start.6 = (f32[16,2048]{1,0:T(8,128)}, f32[16,2048]{1,0:T(8,128)S(1)}, u32[]{:S(2)}) copy-start(f32[16,2048]{1,0:T(8,128)S(1)} %slice_add_fusion) | copy-start | bytes 393220
  40.8 9.6 %collective-permute-start.4 = (f32[16,2048]{1,0:T(8,128)S(1)}, f32[16,2048]{1,0:T(8,128)S(1)}, u32[]{:S(2)}, u32[]{:S(2)}) collective-permute-start(f32[16,2048]{1,0:T(8,128)S(1)} %slice_add_fusion), channel_id=1, source_target_pairs={{2,0},{4,2},{6,4},{8,6},{10,8},{12,10},{14,12},{16,14},{18,16},{20... | collective-permute-start | bytes 393224 | tf_op jit(solution)/shard_map/ppermute | solution.py:80
  42.9 4.9 %copy-start.2 = (bf16[2,2,4,128,1024]{4,3,1,2,0:T(8,128)(2,1)S(1)}, bf16[2,2,4,128,1024]{4,3,1,2,0:T(8,128)(2,1)}, u32[]{:S(2)}) copy-start(bf16[2,2,4,128,1024]{4,3,1,2,0:T(8,128)(2,1)} %get-tuple-element.4) | copy-start | bytes 12582916
  50.5 45.5 %collective-permute-start.5 = (bf16[16,2048]{1,0:T(8,128)(2,1)S(1)}, bf16[16,2048]{1,0:T(8,128)(2,1)S(1)}, u32[]{:S(2)}, u32[]{:S(2)}) collective-permute-start(bf16[16,2048]{1,0:T(8,128)(2,1)S(1)} %add_convert_fusion.1), channel_id=1, source_target_pairs={{0,1},{1,0},{2,3},{3,2},{4,5},{5,4},{6,7},{7,6},{8,9},{9,8},{10,11... | collective-permute-start | bytes 196616 | tf_op jit(solution)/shard_map/ppermute | solution.py:41
  54.0 49.0 %collective-permute-start.16 = (bf16[512,1024]{1,0:T(8,128)(2,1)S(1)}, bf16[512,1024]{1,0:T(8,128)(2,1)S(1)}, u32[]{:S(2)}, u32[]{:S(2)}) collective-permute-start(bf16[512,1024]{1,0:T(8,128)(2,1)S(1)} %convolution_convert_fusion.4), channel_id=1, source_target_pairs={{0,2},{2,0},{4,6},{6,4},{8,10},{10,8},{12,14},{14,12},{16,18},{18,... | collective-permute-start | bytes 3145736 | tf_op jit(solution)/shard_map/ppermute | solution.py:49
  57.0 2.2 %copy-start.5 = (bf16[2,2,4,128,1024]{4,3,2,1,0:T(8,128)(2,1)S(1)}, bf16[2,2,4,128,1024]{4,3,2,1,0:T(8,128)(2,1)}, u32[]{:S(2)}) copy-start(bf16[2,2,4,128,1024]{4,3,2,1,0:T(8,128)(2,1)} %copy.28) | copy-start | bytes 12582916
  58.1 48.3 %collective-permute-start.10 = (bf16[512,1024]{1,0:T(8,128)(2,1)S(1)}, bf16[512,1024]{1,0:T(8,128)(2,1)S(1)}, u32[]{:S(2)}, u32[]{:S(2)}) collective-permute-start(bf16[512,1024]{1,0:T(8,128)(2,1)S(1)} %convolution_convert_fusion.6), channel_id=1, source_target_pairs={{0,2},{2,0},{4,6},{6,4},{8,10},{10,8},{12,14},{14,12},{16,18},{18,... | collective-permute-start | bytes 3145736 | tf_op jit(solution)/shard_map/ppermute | solution.py:49
  59.2 2.2 %copy-start.4 = (bf16[2,2,4,128,1024]{4,3,2,1,0:T(8,128)(2,1)S(1)}, bf16[2,2,4,128,1024]{4,3,2,1,0:T(8,128)(2,1)}, u32[]{:S(2)}) copy-start(bf16[2,2,4,128,1024]{4,3,2,1,0:T(8,128)(2,1)} %copy.29) | copy-start | bytes 12582916
  99.2 8.2 %collective-permute-start.14 = (bf16[512,1024]{1,0:T(8,128)(2,1)S(1)}, bf16[512,1024]{1,0:T(8,128)(2,1)S(1)}, u32[]{:S(2)}, u32[]{:S(2)}) collective-permute-start(bf16[512,1024]{1,0:T(8,128)(2,1)S(1)} %convolution_convert_fusion.5), channel_id=1, source_target_pairs={{0,2},{2,0},{4,6},{6,4},{8,10},{10,8},{12,14},{14,12},{16,18},{18,... | collective-permute-start | bytes 3145736 | tf_op jit(solution)/shard_map/ppermute | solution.py:49
  102.4 8.6 %collective-permute-start.8 = (bf16[512,1024]{1,0:T(8,128)(2,1)S(1)}, bf16[512,1024]{1,0:T(8,128)(2,1)S(1)}, u32[]{:S(2)}, u32[]{:S(2)}) collective-permute-start(bf16[512,1024]{1,0:T(8,128)(2,1)S(1)} %convolution_convert_fusion.7), channel_id=1, source_target_pairs={{0,2},{2,0},{4,6},{6,4},{8,10},{10,8},{12,14},{14,12},{16,18},{18,... | collective-permute-start | bytes 3145736 | tf_op jit(solution)/shard_map/ppermute | solution.py:49
  104.1 15.1 %collective-permute-start.17 = (bf16[2,128,1024]{2,1,0:T(8,128)(2,1)S(1)}, bf16[2,128,1024]{2,1,0:T(8,128)(2,1)S(1)}, u32[]{:S(2)}, u32[]{:S(2)}) collective-permute-start(bf16[2,128,1024]{2,1,0:T(8,128)(2,1)S(1)} %fusion.35), channel_id=1, source_target_pairs={{0,4},{2,6},{4,0},{6,2},{8,12},{10,14},{12,8},{14,10},{16,20},{18,... | collective-permute-start | bytes 1572872 | tf_op jit(solution)/shard_map/ppermute | solution.py:49
  108.8 21.6 %collective-permute-start.15 = (bf16[2,128,1024]{2,1,0:T(8,128)(2,1)S(1)}, bf16[2,128,1024]{2,1,0:T(8,128)(2,1)S(1)}, u32[]{:S(2)}, u32[]{:S(2)}) collective-permute-start(bf16[2,128,1024]{2,1,0:T(8,128)(2,1)S(1)} %fusion.34), channel_id=1, source_target_pairs={{0,4},{2,6},{4,0},{6,2},{8,12},{10,14},{12,8},{14,10},{16,20},{18,... | collective-permute-start | bytes 1572872 | tf_op jit(solution)/shard_map/ppermute | solution.py:49
  109.0 32.7 %collective-permute-start.11 = (bf16[2,128,1024]{2,1,0:T(8,128)(2,1)S(1)}, bf16[2,128,1024]{2,1,0:T(8,128)(2,1)S(1)}, u32[]{:S(2)}, u32[]{:S(2)}) collective-permute-start(bf16[2,128,1024]{2,1,0:T(8,128)(2,1)S(1)} %fusion.37), channel_id=1, source_target_pairs={{0,4},{2,6},{4,0},{6,2},{8,12},{10,14},{12,8},{14,10},{16,20},{18,... | collective-permute-start | bytes 1572872 | tf_op jit(solution)/shard_map/ppermute | solution.py:49
  112.2 40.1 %collective-permute-start.9 = (bf16[2,128,1024]{2,1,0:T(8,128)(2,1)S(1)}, bf16[2,128,1024]{2,1,0:T(8,128)(2,1)S(1)}, u32[]{:S(2)}, u32[]{:S(2)}) collective-permute-start(bf16[2,128,1024]{2,1,0:T(8,128)(2,1)S(1)} %fusion.36), channel_id=1, source_target_pairs={{0,4},{2,6},{4,0},{6,2},{8,12},{10,14},{12,8},{14,10},{16,20},{18,... | collective-permute-start | bytes 1572872 | tf_op jit(solution)/shard_map/ppermute | solution.py:49
  131.1 26.0 %collective-permute-start.18 = (bf16[2,128,1024]{2,1,0:T(8,128)(2,1)S(1)}, bf16[2,128,1024]{2,1,0:T(8,128)(2,1)S(1)}, u32[]{:S(2)}, u32[]{:S(2)}) collective-permute-start(bf16[2,128,1024]{2,1,0:T(8,128)(2,1)S(1)} %fusion.38), channel_id=1, source_target_pairs={{0,8},{2,10},{4,12},{6,14},{8,0},{10,2},{12,4},{14,6},{16,24},{18,... | collective-permute-start | bytes 1572872 | tf_op jit(solution)/shard_map/ppermute | solution.py:49
  152.9 19.6 %collective-permute-start.12 = (bf16[2,128,1024]{2,1,0:T(8,128)(2,1)S(1)}, bf16[2,128,1024]{2,1,0:T(8,128)(2,1)S(1)}, u32[]{:S(2)}, u32[]{:S(2)}) collective-permute-start(bf16[2,128,1024]{2,1,0:T(8,128)(2,1)S(1)} %fusion.33), channel_id=1, source_target_pairs={{0,8},{2,10},{4,12},{6,14},{8,0},{10,2},{12,4},{14,6},{16,24},{18,... | collective-permute-start | bytes 1572872 | tf_op jit(solution)/shard_map/ppermute | solution.py:49
  157.4 20.3 %collective-permute-start.19 = (bf16[1,128,1024]{2,1,0:T(8,128)(2,1)S(1)}, bf16[1,128,1024]{2,1,0:T(8,128)(2,1)S(1)}, u32[]{:S(2)}, u32[]{:S(2)}) collective-permute-start(bf16[1,128,1024]{2,1,0:T(8,128)(2,1)S(1)} %dynamic-slice_convert_fusion.1), channel_id=1, source_target_pairs={{0,16},{2,18},{4,20},{6,22},{8,24},{10,26},{12,28},{14,30},{16,0},... | collective-permute-start | bytes 786440 | tf_op jit(solution)/shard_map/ppermute | solution.py:49
  172.7 13.7 %collective-permute-start.13 = (bf16[1,128,1024]{2,1,0:T(8,128)(2,1)S(1)}, bf16[1,128,1024]{2,1,0:T(8,128)(2,1)S(1)}, u32[]{:S(2)}, u32[]{:S(2)}) collective-permute-start(bf16[1,128,1024]{2,1,0:T(8,128)(2,1)S(1)} %dynamic-slice_convert_fusion.2), channel_id=1, source_target_pairs={{0,16},{2,18},{4,20},{6,22},{8,24},{10,26},{12,28},{14,30},{16,0},... | collective-permute-start | bytes 786440 | tf_op jit(solution)/shard_map/ppermute | solution.py:49
where the time goes:
time: 188 us
  waiting for transfers between devices  108 us (57%)
  matrix products  28.3 us (15%)
  starting transfers between devices  26.2 us (14%)
  local copies, waits for them, and re-layouts  20.3 us (11%)
  other arithmetic  3.64 us (2%)
    ppermute x12, waiting for transfers between devices, shift_dp(): return lax.ppermute(x, 'dp', moves)  58.1 us
    ppermute x3, waiting for transfers between devices, shift_tensor(): lax.ppermute(x, 'tensor', [(t, (t + r) % parts) for t in range(parts)])  32.8 us
    ppermute x5, waiting for transfers between devices, later(): return lax.ppermute(x, 'dp', [(i, i - r) for i in range(r, count)])  17 us
    ppermute x12, starting transfers between devices, shift_dp(): return lax.ppermute(x, 'dp', moves)  15.5 us
    transpose x3, local copies, waits for them, and re-layouts, body(): proj[:, :, :, lo:hi].transpose(0, 2, 1, 3, 4).reshape(parts, -1, heads)  11.2 us
    dot_general x8, matrix products, of_core(): lax.dot_general(lhs, attn_out, (((0,), (0,)), ((), ())), preferred_elemen...  8.51 us
    dot_general x4, matrix products, body(): term = jnp.dot(z, w, preferred_element_type=F32)  8.46 us
    unnamed x43, local copies, waits for them, and re-layouts  7.69 us
  transfers between devices with their start and end apart: 20, of which 10 were waited for; matrix products, arithmetic and copies ran while one was open for 24% of the time, Pallas kernels for 0%

commit v1 on v0

--- a/solution.py
+++ b/solution.py
@@ -1,6 +1,7 @@
 import jax
 import jax.numpy as jnp
 from jax import lax
+from jax.experimental import pallas as pl
 from jax.sharding import PartitionSpec as P
 
 F32 = jnp.float32
@@ -20,6 +21,10 @@
     if rows % 128 or rows == 128:
         return [(0, rows)]
     return [(0, rows // 2), (rows // 2, rows)]
+
+
+def copy_block(src, dst):
+    dst[...] = src[...]
 
 
 def body(attn_out, out_proj_t, grad_out, read_weights, memory_gate, write_pos):
@@ -51,6 +56,21 @@
     cuts = cuts_of(rows)
 
     def columns(x, lo, hi):
+        size = hi - lo
+        n = x.shape[0]
+        if size % 128 == 0:
+            per = rows // size
+            return pl.pallas_call(
+                copy_block,
+                grid=(cores, pairs),
+                in_specs=[
+                    pl.BlockSpec(
+                        (n, size), lambda c, p: (0, (p * cores + c) * per + lo // size)
+                    )
+                ],
+                out_specs=pl.BlockSpec((n, size), lambda c, p: (0, c * pairs + p)),
+                out_shape=jax.ShapeDtypeStruct((n, held * size), x.dtype),
+            )(x)
         return jnp.concatenate(
             [
                 x[:, (p * cores + c) * rows + lo : (p * cores + c) * rows + hi]
@@ -148,7 +168,24 @@
             bit *= 2
         return x[0]
 
-    proj = out_proj_t.reshape(parts, pairs, cores, rows, heads)
+    def rows_of(lo, hi):
+        size = hi - lo
+        per = rows // size
+        return pl.pallas_call(
+            copy_block,
+            grid=(parts, cores, pairs),
+            in_specs=[
+                pl.BlockSpec(
+                    (size, heads),
+                    lambda t, c, p: (((t * pairs + p) * cores + c) * per + lo // size, 0),
+                )
+            ],
+            out_specs=pl.BlockSpec(
+                (size, heads), lambda t, c, p: ((t * cores + c) * pairs + p, 0)
+            ),
+            out_shape=jax.ShapeDtypeStruct((parts * held * size, heads), out_proj_t.dtype),
+        )(out_proj_t)
+
     z_own, near_own, row_cuts = [], [], []
     for k, (lo, hi) in enumerate(cuts):
         row_cuts.append([columns(x, lo, hi) for x in [fresh] + fresh_got])
@@ -160,7 +197,7 @@
         z_got = [put_rows(x, y) for x, y in zip(got[k], row_cuts[k][1:])]
         near = [near_own[k]] + [near_sum(z, hi - lo) for z in z_got]
         sums.append(deep_sum(jnp.concatenate(ordered(near), axis=0)))
-        w_cut = proj[:, :, :, lo:hi].transpose(0, 2, 1, 3, 4).reshape(parts, -1, heads)
+        w_cut = rows_of(lo, hi).reshape(parts, -1, heads)
         for r, z in enumerate([z_own[k]] + z_got):
             w = lax.dynamic_index_in_dim(w_cut, (side - r) % parts, 0, keepdims=False)
             term = jnp.dot(z, w, preferred_element_type=F32)

time: 188 us -> 208 us (1.11)
  Pallas kernels: 0 us -> 47.1 us
  local copies, waits for them, and re-layouts: 20.3 us -> 2.19 us
  waiting for transfers between devices: 108 us -> 90 us
  matrix products: 28.3 us -> 36.9 us
    pallas_call x0 -> x8, Pallas kernels: none -> 47.1 us  [the longest x6 26.6 us: columns(): pl.pallas_call(copy_block, grid=(cores, pairs), in_specs=[pl.BlockSpec((n...]
    ppermute x3, waiting for transfers between devices: 32.8 us -> 14.7 us  [shift_tensor(): lax.ppermute(x, 'tensor', [(t, (t + r) % parts) for t in range(parts)])]
    transpose x3 -> x0, local copies, waits for them, and re-layouts: 11.2 us -> none  [body(): proj[:, :, :, lo:hi].transpose(0, 2, 1, 3, 4).reshape(parts, -1, heads)]
    unnamed x43 -> x37, local copies, waits for them, and re-layouts: 7.69 us -> 1.65 us
    dot_general x8, matrix products: 8.51 us -> 12.6 us  [of_core(): lax.dot_general(lhs, attn_out, (((0,), (0,)), ((), ())), preferred_elemen...]
    dot_general x4, matrix products: 8.46 us -> 11.8 us  [body(): term = jnp.dot(z, w, preferred_element_type=F32)]
  transfers between devices with their start and end apart: 20 -> 20, of which waited for: 10 -> 10; matrix products, arithmetic and copies ran while one was open for 24% -> 18% of each run, Pallas kernels for 0% -> 23%
where the time goes in v1:
time: 208 us; the launch traced here: 206 us
  waiting for transfers between devices  90 us (43%)
  Pallas kernels  47.1 us (23%)
  matrix products  36.9 us (18%)
  starting transfers between devices  24.4 us (12%)
  other arithmetic  4.62 us (2%)
  local copies, waits for them, and re-layouts  2.19 us (1%)
    ppermute x12, waiting for transfers between devices, shift_dp(): return lax.ppermute(x, 'dp', moves)  56.8 us
    pallas_call x6, Pallas kernels, columns(): pl.pallas_call(copy_block, grid=(cores, pairs), in_specs=[pl.BlockSpec((n...  26.6 us
    pallas_call x2, Pallas kernels, rows_of(): pl.pallas_call(copy_block, grid=(parts, cores, pairs), in_specs=[pl.Block...  20.5 us
    ppermute x5, waiting for transfers between devices, later(): return lax.ppermute(x, 'dp', [(i, i - r) for i in range(r, count)])  18.5 us
    ppermute x3, waiting for transfers between devices, shift_tensor(): lax.ppermute(x, 'tensor', [(t, (t + r) % parts) for t in range(parts)])  14.7 us
    ppermute x12, starting transfers between devices, shift_dp(): return lax.ppermute(x, 'dp', moves)  14.4 us
    dot_general x8, matrix products, of_core(): lax.dot_general(lhs, attn_out, (((0,), (0,)), ((), ())), preferred_elemen...  12.6 us
    dot_general x4, matrix products, body(): term = jnp.dot(z, w, preferred_element_type=F32)  11.8 us
  transfers between devices with their start and end apart: 20, of which 10 were waited for; matrix products, arithmetic and copies ran while one was open for 18% of the time, Pallas kernels for 23%

profile of v1, /device:TPU:0, one launch (start us, length us, event | category | flops | bytes accessed | tf_op | source)
XLA Modules:
  0.0 206.3 jit_solution(8278412380577354621)
XLA Ops:
  1.6 2.6 %fusion.39 = f32[48,2048]{1,0:T(8,128)S(1)} fusion(bf16[768,2048]{1,0:T(8,128)(2,1)} %src.6, bf16[768,16]{0,1:T(8,128)(2,1)S(1)} %get-tuple-element.8, bf16[768,16]{0,1:T(8,128)(2,1)S(1)} %get-tuple-element.9, bf16[768,16]{0,1:T(8,128)(2,1)S(1)} %get-tuple-element.7), kind=kOutput, calls=%fused_computation.79 | convolution fusion | flops 151216128 | bytes 3612672 | tf_op jit(solution)/shard_map/dot_general | solution.py:91
  4.3 1.3 collective-permute-start
  5.6 2.0 collective-permute-done
  7.9 1.3 collective-permute-start.1
  9.2 7.9 %collective-permute-done.1 = f32[16,2176]{1,0:T(8,128)S(1)} collective-permute-done((f32[16,2176]{1,0:T(8,128)S(1)}, f32[16,2176]{1,0:T(8,128)S(1)}, u32[]{:S(2)}, u32[]{:S(2)}) %collective-permute-start.1) | collective-permute-done | bytes 139296 | tf_op jit(solution)/shard_map/ppermute | solution.py:100
  17.3 1.3 collective-permute-start.2
  18.6 8.7 %collective-permute-done.2 = f32[16,2176]{1,0:T(8,128)S(1)} collective-permute-done((f32[16,2176]{1,0:T(8,128)S(1)}, f32[16,2176]{1,0:T(8,128)S(1)}, u32[]{:S(2)}, u32[]{:S(2)}) %collective-permute-start.2) | collective-permute-done | bytes 139296 | tf_op jit(solution)/shard_map/ppermute | solution.py:100
  27.5 1.3 collective-permute-start.3
  28.8 5.5 %shard_map.86 = bf16[768,1024]{1,0:T(8,128)(2,1)} custom-call(bf16[768,2048]{1,0:T(8,128)(2,1)} %src.6), custom_call_target="tpu_custom_call" | custom-call | tf_op jit(solution)/shard_map/pallas_call | solution.py:63
  34.3 1.5 collective-permute-start.6
  35.8 5.4 %shard_map.90 = bf16[768,1024]{1,0:T(8,128)(2,1)} custom-call(bf16[768,2048]{1,0:T(8,128)(2,1)} %src.6), custom_call_target="tpu_custom_call" | custom-call | tf_op jit(solution)/shard_map/pallas_call | solution.py:63
  42.1 1.3 collective-permute-start.4
  43.4 2.4 %fusion.46 = f32[16,2048]{1,0:T(8,128)S(1)} fusion(bf16[768,2048]{1,0:T(8,128)(2,1)} %src.6, s32[16]{0:T(128)S(1)} %bitcast.132), kind=kOutput, calls=%fused_computation.91 | convolution fusion | flops 50343936 | bytes 3276864 | tf_op jit(solution)/shard_map/dot_general | solution.py:117
  45.9 10.2 %shard_map.87 = bf16[2048,1024]{1,0:T(8,128)(2,1)} custom-call(bf16[4096,1024]{1,0:T(8,128)(2,1)} %src.7), custom_call_target="tpu_custom_call" | custom-call | tf_op jit(solution)/shard_map/pallas_call | solution.py:174
  56.1 10.3 %shard_map.91 = bf16[2048,1024]{1,0:T(8,128)(2,1)} custom-call(bf16[4096,1024]{1,0:T(8,128)(2,1)} %src.7), custom_call_target="tpu_custom_call" | custom-call | tf_op jit(solution)/shard_map/pallas_call | solution.py:174
  67.1 3.9 %shard_map.85 = bf16[16,1024]{1,0:T(8,128)(2,1)} custom-call(bf16[16,2048]{1,0:T(8,128)(2,1)} %add_convert_fusion.1.src), custom_call_target="tpu_custom_call" | custom-call | tf_op jit(solution)/shard_map/pallas_call | solution.py:63
  71.1 1.5 collective-permute-start.5
  72.5 3.9 %shard_map.89 = bf16[16,1024]{1,0:T(8,128)(2,1)} custom-call(bf16[16,2048]{1,0:T(8,128)(2,1)} %add_convert_fusion.1.src), custom_call_target="tpu_custom_call" | custom-call | tf_op jit(solution)/shard_map/pallas_call | solution.py:63
  76.5 1.4 broadcast_select_fusion.3
  78.0 2.0 convolution_convert_fusion.6
  81.6 2.0 convolution_convert_fusion.4
  84.1 3.5 %fusion.7 = f32[768,1024]{1,0:T(8,128)} fusion(bf16[768,1024]{1,0:T(8,128)(2,1)S(1)} %broadcast_select_fusion.3, bf16[2,1024,1024]{2,1,0:T(8,128)(2,1)S(1)} %bitcast.121, s32[]{:T(128)S(6)} %select_n.154), kind=kOutput, calls=%fused_computation.11 | convolution fusion | flops 1610612736 | bytes 6815748 | tf_op jit(solution)/shard_map/dot_general | solution.py:203
  87.6 3.5 %fusion.3 = f32[768,1024]{1,0:T(8,128)} fusion(bf16[768,1024]{1,0:T(8,128)(2,1)S(1)} %broadcast_select_fusion.1, bf16[2,1024,1024]{2,1,0:T(8,128)(2,1)S(1)} %bitcast.119, s32[]{:T(128)S(6)} %select_n.154), kind=kOutput, calls=%fused_computation.7 | convolution fusion | flops 1610612736 | bytes 6815748 | tf_op jit(solution)/shard_map/dot_general | solution.py:203
  91.1 14.7 %collective-permute-done.5.src = bf16[16,2048]{1,0:T(8,128)(2,1)S(1)} collective-permute-done((bf16[16,2048]{1,0:T(8,128)(2,1)}, bf16[16,2048]{1,0:T(8,128)(2,1)S(1)}, u32[]{:S(2)}, u32[]{:S(2)}) %collective-permute-start.5) | collective-permute-done | bytes 65568 | tf_op jit(solution)/shard_map/ppermute | solution.py:46
  106.4 3.9 %shard_map.88 = bf16[16,1024]{1,0:T(8,128)(2,1)} custom-call(bf16[16,2048]{1,0:T(8,128)(2,1)} %copy-done.9), custom_call_target="tpu_custom_call" | custom-call | tf_op jit(solution)/shard_map/pallas_call | solution.py:63
  110.4 3.9 %shard_map.92 = bf16[16,1024]{1,0:T(8,128)(2,1)} custom-call(bf16[16,2048]{1,0:T(8,128)(2,1)} %copy-done.9), custom_call_target="tpu_custom_call" | custom-call | tf_op jit(solution)/shard_map/pallas_call | solution.py:63
  114.3 2.1 %broadcast_select_fusion.2 = bf16[768,1024]{1,0:T(8,128)(2,1)S(1)} fusion(bf16[768,1024]{1,0:T(8,128)(2,1)} %collective-permute-done.6, pred[768]{0:T(1024)(128)(4,1)S(1)} %fusion.47, bf16[16,1024]{1,0:T(8,128)(2,1)} %shard_map.88, s32[16]{0:T(128)S(1)} %bitcast.136), kind=kOutput, calls=%fused_computation.27 | convolution fusion | flops 26750976 | bytes 3179328 | tf_op jit(solution)/shard_map/dot_general | solution.py:133
  117.5 2.1 %broadcast_select_fusion = bf16[768,1024]{1,0:T(8,128)(2,1)S(1)} fusion(bf16[768,1024]{1,0:T(8,128)(2,1)} %collective-permute-done.7, pred[768]{0:T(1024)(128)(4,1)S(1)} %fusion.47, bf16[16,1024]{1,0:T(8,128)(2,1)S(1)} %copy-done.10, s32[16]{0:T(128)S(1)} %bitcast.137), kind=kOutput, calls=%fused_computation.25 | convolution fusion | flops 26750976 | bytes 3179328 | tf_op jit(solution)/shard_map/dot_general | solution.py:133
  119.6 1.0 convolution_convert_fusion.5
  121.2 2.2 %convert_add_fusion.2 = f32[512,1024]{1,0:T(8,128)S(1)} fusion(bf16[512,1024]{1,0:T(8,128)(2,1)} %collective-permute-done.10, bf16[768,1024]{1,0:T(8,128)(2,1)S(1)} %copy-done, bf16[768,1024]{1,0:T(8,128)(2,1)S(1)} %copy-done.8, s32[]{:T(128)S(6)} %select_n.162), kind=kOutput, calls=%fused_computation.15 | convolution fusion | flops 806354944 | bytes 5505028 | tf_op jit(solution)/shard_map/dot_general | solution.py:141
  123.5 1.5 collective-permute-start.11
  125.0 2.2 %convert_add_fusion = f32[512,1024]{1,0:T(8,128)S(1)} fusion(bf16[512,1024]{1,0:T(8,128)(2,1)} %collective-permute-done.16, bf16[768,1024]{1,0:T(8,128)(2,1)S(1)} %copy-done, bf16[768,1024]{1,0:T(8,128)(2,1)S(1)} %broadcast_select_fusion.1, s32[]{:T(128)S(6)} %select_n.162), kind=kOutput, calls=%fused_computation.13 | convolution fusion | flops 806354944 | bytes 5505028 | tf_op jit(solution)/shard_map/dot_general | solution.py:141
  127.3 1.0 convert_add_fusion.3
  129.2 1.5 collective-permute-start.17
  130.6 1.0 convert_add_fusion.1
  132.4 6.0 %collective-permute-done.11 = bf16[2,128,1024]{2,1,0:T(8,128)(2,1)S(1)} collective-permute-done((bf16[2,128,1024]{2,1,0:T(8,128)(2,1)S(1)}, bf16[2,128,1024]{2,1,0:T(8,128)(2,1)S(1)}, u32[]{:S(2)}, u32[]{:S(2)}) %collective-permute-start.11) | collective-permute-done | bytes 524320 | tf_op jit(solution)/shard_map/ppermute | solution.py:54
  138.4 11.2 %collective-permute-done.9 = bf16[2,128,1024]{2,1,0:T(8,128)(2,1)S(1)} collective-permute-done((bf16[2,128,1024]{2,1,0:T(8,128)(2,1)S(1)}, bf16[2,128,1024]{2,1,0:T(8,128)(2,1)S(1)}, u32[]{:S(2)}, u32[]{:S(2)}) %collective-permute-start.9) | collective-permute-done | bytes 524320 | tf_op jit(solution)/shard_map/ppermute | solution.py:54
  150.5 1.5 collective-permute-start.12
  152.0 8.9 %collective-permute-done.17 = bf16[2,128,1024]{2,1,0:T(8,128)(2,1)S(1)} collective-permute-done((bf16[2,128,1024]{2,1,0:T(8,128)(2,1)S(1)}, bf16[2,128,1024]{2,1,0:T(8,128)(2,1)S(1)}, u32[]{:S(2)}, u32[]{:S(2)}) %collective-permute-start.17) | collective-permute-done | bytes 524320 | tf_op jit(solution)/shard_map/ppermute | solution.py:54
  160.9 10.6 %collective-permute-done.15 = bf16[2,128,1024]{2,1,0:T(8,128)(2,1)S(1)} collective-permute-done((bf16[2,128,1024]{2,1,0:T(8,128)(2,1)S(1)}, bf16[2,128,1024]{2,1,0:T(8,128)(2,1)S(1)}, u32[]{:S(2)}, u32[]{:S(2)}) %collective-permute-start.15) | collective-permute-done | bytes 524320 | tf_op jit(solution)/shard_map/ppermute | solution.py:54
  172.3 1.5 collective-permute-start.18
  174.1 1.8 fusion.5
  176.1 3.3 %collective-permute-start.13 = (bf16[1,128,1024]{2,1,0:T(8,128)(2,1)S(1)}, bf16[1,128,1024]{2,1,0:T(8,128)(2,1)S(1)}, u32[]{:S(2)}, u32[]{:S(2)}) collective-permute-start(bf16[1,128,1024]{2,1,0:T(8,128)(2,1)S(1)} %dynamic-slice_convert_fusion.2), channel_id=1, source_target_pairs={{0,16},{2,18},{4,20},{6,22},{8,24},{10,26},{12,28},{14,30},{16,0},... | collective-permute-start | bytes 786440 | tf_op jit(solution)/shard_map/ppermute | solution.py:54
  179.5 11.7 %collective-permute-done.18 = bf16[2,128,1024]{2,1,0:T(8,128)(2,1)S(1)} collective-permute-done((bf16[2,128,1024]{2,1,0:T(8,128)(2,1)S(1)}, bf16[2,128,1024]{2,1,0:T(8,128)(2,1)S(1)}, u32[]{:S(2)}, u32[]{:S(2)}) %collective-permute-start.18) | collective-permute-done | bytes 524320 | tf_op jit(solution)/shard_map/ppermute | solution.py:54
  191.4 2.3 %collective-permute-start.19 = (bf16[1,128,1024]{2,1,0:T(8,128)(2,1)S(1)}, bf16[1,128,1024]{2,1,0:T(8,128)(2,1)S(1)}, u32[]{:S(2)}, u32[]{:S(2)}) collective-permute-start(bf16[1,128,1024]{2,1,0:T(8,128)(2,1)S(1)} %dynamic-slice_convert_fusion.1), channel_id=1, source_target_pairs={{0,16},{2,18},{4,20},{6,22},{8,24},{10,26},{12,28},{14,30},{16,0},... | collective-permute-start | bytes 786440 | tf_op jit(solution)/shard_map/ppermute | solution.py:54
  193.7 3.0 %add_convert_fusion = bf16[768,1024]{1,0:T(8,128)(2,1)} fusion(f32[768,1024]{1,0:T(8,128)S(1)} %copy-done.17, f32[768,1024]{1,0:T(8,128)S(1)} %copy-done.16, f32[768,1024]{1,0:T(8,128)S(1)} %fusion.5, bf16[768,1024]{1,0:T(8,128)(2,1)S(1)} %broadcast_select_fusion, bf16[2,1024,1024]{2,1,0:T(8,128)(2,1)S(1)} %bitcast.120, s32[]{:T(128)S(6)} %select_n.157), kind=kOutput, calls=%fused_computation.2 | convolution fusion | flops 1613758464 | bytes 14680068 | tf_op jit(solution)/shard_map/dot_general | solution.py:203
  196.8 8.3 %collective-permute-done.19 = bf16[1,128,1024]{2,1,0:T(8,128)(2,1)S(1)} collective-permute-done((bf16[1,128,1024]{2,1,0:T(8,128)(2,1)S(1)}, bf16[1,128,1024]{2,1,0:T(8,128)(2,1)S(1)}, u32[]{:S(2)}, u32[]{:S(2)}) %collective-permute-start.19) | collective-permute-done | bytes 262176 | tf_op jit(solution)/shard_map/ppermute | solution.py:54
  205.2 1.0 pad_maximum_fusion.2
  (84 shorter events, 11.9 us)
Async XLA Ops:
  0.6 77.3 %copy-start = (bf16[768,1024]{1,0:T(8,128)(2,1)S(1)}, bf16[768,1024]{1,0:T(8,128)(2,1)}, u32[]{:S(2)}) copy-start(bf16[768,1024]{1,0:T(8,128)(2,1)} %param.6) | copy-start | bytes 4718596
  1.6 2.6 %copy-start.13 = (f32[16,16]{1,0:T(8,128)S(1)}, f32[16,16]{1,0:T(8,128)}, u32[]{:S(2)}) copy-start(f32[16,16]{1,0:T(8,128)} %param.10) | copy-start | bytes 3076
  1.6 15.5 %copy-start.14 = (pred[2176]{0:T(1024)(128)(4,1)S(1)}, pred[2176]{0:T(1024)(128)(4,1)}, u32[]{:S(2)}) copy-start(pred[2176]{0:T(1024)(128)(4,1)} %constant.159.clone.1) | copy-start | bytes 6532
  4.3 3.3 %collective-permute-start = (f32[16,2176]{1,0:T(8,128)S(1)}, f32[16,2176]{1,0:T(8,128)S(1)}, u32[]{:S(2)}, u32[]{:S(2)}) collective-permute-start(f32[16,2176]{1,0:T(8,128)S(1)} %select_maximum_fusion), channel_id=1, source_target_pairs={{2,0},{4,2},{6,4},{8,6},{10,8},{12,10},{14,12},{16,14},{18,16},{20... | collective-permute-start | bytes 417800 | tf_op jit(solution)/shard_map/ppermute | solution.py:100
  7.9 9.2 %collective-permute-start.1 = (f32[16,2176]{1,0:T(8,128)S(1)}, f32[16,2176]{1,0:T(8,128)S(1)}, u32[]{:S(2)}, u32[]{:S(2)}) collective-permute-start(f32[16,2176]{1,0:T(8,128)S(1)} %fusion), channel_id=1, source_target_pairs={{4,0},{6,2},{8,4},{10,6},{12,8},{14,10},{16,12},{18,14},{20,16},{2... | collective-permute-start | bytes 417800 | tf_op jit(solution)/shard_map/ppermute | solution.py:100
  17.3 10.0 %collective-permute-start.2 = (f32[16,2176]{1,0:T(8,128)S(1)}, f32[16,2176]{1,0:T(8,128)S(1)}, u32[]{:S(2)}, u32[]{:S(2)}) collective-permute-start(f32[16,2176]{1,0:T(8,128)S(1)} %select_add_fusion.1), channel_id=1, source_target_pairs={{8,0},{10,2},{12,4},{14,6},{16,8},{18,10},{20,12},{22,14},{24,16},... | collective-permute-start | bytes 417800 | tf_op jit(solution)/shard_map/ppermute | solution.py:100
  27.5 14.2 %collective-permute-start.3 = (f32[16,2176]{1,0:T(8,128)S(1)}, f32[16,2176]{1,0:T(8,128)S(1)}, u32[]{:S(2)}, u32[]{:S(2)}) collective-permute-start(f32[16,2176]{1,0:T(8,128)S(1)} %select_add_fusion), channel_id=1, source_target_pairs={{16,0},{18,2},{20,4},{22,6},{24,8},{26,10},{28,12},{30,14},{17,1},... | collective-permute-start | bytes 417800 | tf_op jit(solution)/shard_map/ppermute | solution.py:100
  34.3 7.7 %slice-start = ((pred[2176]{0:T(1024)(128)(4,1)}), pred[2048]{0:T(1024)(128)(4,1)S(1)}, s32[]{:S(2)}) async-start(pred[2176]{0:T(1024)(128)(4,1)} %constant.159.clone.1), calls=%async_computation | async-start | bytes 4096 | tf_op jit(solution)/shard_map/slice | solution.py:110
  34.3 9.1 %copy-start.15 = (s32[1,16]{1,0:T(1,128)S(1)}, s32[1,16]{1,0:T(1,128)}, u32[]{:S(2)}) copy-start(s32[1,16]{1,0:T(1,128)} %param.11) | copy-start | bytes 196
  34.3 79.9 %collective-permute-start.6 = (bf16[768,1024]{1,0:T(8,128)(2,1)}, bf16[768,1024]{1,0:T(8,128)(2,1)}, u32[]{:S(2)}, u32[]{:S(2)}) collective-permute-start(bf16[768,1024]{1,0:T(8,128)(2,1)} %shard_map.86), channel_id=1, source_target_pairs={{0,1},{1,0},{2,3},{3,2},{4,5},{5,4},{6,7},{7,6},{8,9},{9,8},{10,11... | collective-permute-start | bytes 4718600 | tf_op jit(solution)/shard_map/ppermute | solution.py:46
  41.2 76.3 %collective-permute-start.7 = (bf16[768,1024]{1,0:T(8,128)(2,1)}, bf16[768,1024]{1,0:T(8,128)(2,1)}, u32[]{:S(2)}, u32[]{:S(2)}) collective-permute-start(bf16[768,1024]{1,0:T(8,128)(2,1)} %shard_map.90), channel_id=1, source_target_pairs={{0,1},{1,0},{2,3},{3,2},{4,5},{5,4},{6,7},{7,6},{8,9},{9,8},{10,11... | collective-permute-start | bytes 4718600 | tf_op jit(solution)/shard_map/ppermute | solution.py:46
  42.1 14.0 %copy-start.12 = (f32[16,2048]{1,0:T(8,128)}, f32[16,2048]{1,0:T(8,128)S(1)}, u32[]{:S(2)}) copy-start(f32[16,2048]{1,0:T(8,128)S(1)} %slice_add_fusion) | copy-start | bytes 393220
  42.1 24.4 %collective-permute-start.4 = (f32[16,2048]{1,0:T(8,128)S(1)}, f32[16,2048]{1,0:T(8,128)S(1)}, u32[]{:S(2)}, u32[]{:S(2)}) collective-permute-start(f32[16,2048]{1,0:T(8,128)S(1)} %slice_add_fusion), channel_id=1, source_target_pairs={{2,0},{4,2},{6,4},{8,6},{10,8},{12,10},{14,12},{16,14},{18,16},{20... | collective-permute-start | bytes 393224 | tf_op jit(solution)/shard_map/ppermute | solution.py:100
  56.1 20.4 %copy-start.2 = (bf16[768,1024]{1,0:T(8,128)(2,1)S(1)}, bf16[768,1024]{1,0:T(8,128)(2,1)}, u32[]{:S(2)}) copy-start(bf16[768,1024]{1,0:T(8,128)(2,1)} %shard_map.86) | copy-start | bytes 4718596
  71.1 34.7 %collective-permute-start.5 = (bf16[16,2048]{1,0:T(8,128)(2,1)}, bf16[16,2048]{1,0:T(8,128)(2,1)S(1)}, u32[]{:S(2)}, u32[]{:S(2)}) collective-permute-start(bf16[16,2048]{1,0:T(8,128)(2,1)} %add_convert_fusion.1.src), channel_id=1, source_target_pairs={{0,1},{1,0},{2,3},{3,2},{4,5},{5,4},{6,7},{7,6},{8,9},{9,8},{10,11... | collective-permute-start | bytes 196616 | tf_op jit(solution)/shard_map/ppermute | solution.py:46
  77.9 5.6 %copy-start.7 = (bf16[768,1024]{1,0:T(8,128)(2,1)}, bf16[768,1024]{1,0:T(8,128)(2,1)S(1)}, u32[]{:S(2)}) copy-start(bf16[768,1024]{1,0:T(8,128)(2,1)S(1)} %broadcast_select_fusion.3) | copy-start | bytes 4718596
  78.0 2.9 %copy-start.1 = (bf16[768,1024]{1,0:T(8,128)(2,1)S(1)}, bf16[768,1024]{1,0:T(8,128)(2,1)}, u32[]{:S(2)}) copy-start(bf16[768,1024]{1,0:T(8,128)(2,1)} %shard_map.90) | copy-start | bytes 4718596
  78.0 2.9 %copy-start.11 = (bf16[16,1024]{1,0:T(8,128)(2,1)S(1)}, bf16[16,1024]{1,0:T(8,128)(2,1)}, u32[]{:S(2)}) copy-start(bf16[16,1024]{1,0:T(8,128)(2,1)} %shard_map.89) | copy-start | bytes 98308
  80.0 41.2 %collective-permute-start.10 = (bf16[512,1024]{1,0:T(8,128)(2,1)}, bf16[512,1024]{1,0:T(8,128)(2,1)}, u32[]{:S(2)}, u32[]{:S(2)}) collective-permute-start(bf16[512,1024]{1,0:T(8,128)(2,1)} %convolution_convert_fusion.6), channel_id=1, source_target_pairs={{0,2},{2,0},{4,6},{6,4},{8,10},{10,8},{12,14},{14,12},{16,18},{18,... | collective-permute-start | bytes 3145736 | tf_op jit(solution)/shard_map/ppermute | solution.py:54
  81.5 2.6 %copy-start.5 = (bf16[2048,1024]{1,0:T(8,128)(2,1)S(1)}, bf16[2048,1024]{1,0:T(8,128)(2,1)}, u32[]{:S(2)}) copy-start(bf16[2048,1024]{1,0:T(8,128)(2,1)} %shard_map.87) | copy-start | bytes 12582916
  83.6 41.5 %collective-permute-start.16 = (bf16[512,1024]{1,0:T(8,128)(2,1)}, bf16[512,1024]{1,0:T(8,128)(2,1)}, u32[]{:S(2)}, u32[]{:S(2)}) collective-permute-start(bf16[512,1024]{1,0:T(8,128)(2,1)} %convolution_convert_fusion.4), channel_id=1, source_target_pairs={{0,2},{2,0},{4,6},{6,4},{8,10},{10,8},{12,14},{14,12},{16,18},{18,... | collective-permute-start | bytes 3145736 | tf_op jit(solution)/shard_map/ppermute | solution.py:54
  84.1 3.5 %copy-start.3 = (bf16[2048,1024]{1,0:T(8,128)(2,1)S(1)}, bf16[2048,1024]{1,0:T(8,128)(2,1)}, u32[]{:S(2)}) copy-start(bf16[2048,1024]{1,0:T(8,128)(2,1)} %shard_map.91) | copy-start | bytes 12582916
  105.8 0.6 copy-start.9
  116.4 1.1 copy-start.10
  117.4 9.8 %collective-permute-start.8 = (bf16[512,1024]{1,0:T(8,128)(2,1)S(1)}, bf16[512,1024]{1,0:T(8,128)(2,1)S(1)}, u32[]{:S(2)}, u32[]{:S(2)}) collective-permute-start(bf16[512,1024]{1,0:T(8,128)(2,1)S(1)} %convolution_convert_fusion.7), channel_id=1, source_target_pairs={{0,2},{2,0},{4,6},{6,4},{8,10},{10,8},{12,14},{14,12},{16,18},{18,... | collective-permute-start | bytes 3145736 | tf_op jit(solution)/shard_map/ppermute | solution.py:54
  119.6 1.6 copy-start.8
  120.7 9.9 %collective-permute-start.14 = (bf16[512,1024]{1,0:T(8,128)(2,1)S(1)}, bf16[512,1024]{1,0:T(8,128)(2,1)S(1)}, u32[]{:S(2)}, u32[]{:S(2)}) collective-permute-start(bf16[512,1024]{1,0:T(8,128)(2,1)S(1)} %convolution_convert_fusion.5), channel_id=1, source_target_pairs={{0,2},{2,0},{4,6},{6,4},{8,10},{10,8},{12,14},{14,12},{16,18},{18,... | collective-permute-start | bytes 3145736 | tf_op jit(solution)/shard_map/ppermute | solution.py:54
  123.5 14.9 %collective-permute-start.11 = (bf16[2,128,1024]{2,1,0:T(8,128)(2,1)S(1)}, bf16[2,128,1024]{2,1,0:T(8,128)(2,1)S(1)}, u32[]{:S(2)}, u32[]{:S(2)}) collective-permute-start(bf16[2,128,1024]{2,1,0:T(8,128)(2,1)S(1)} %fusion.37), channel_id=1, source_target_pairs={{0,4},{2,6},{4,0},{6,2},{8,12},{10,14},{12,8},{14,10},{16,20},{18,... | collective-permute-start | bytes 1572872 | tf_op jit(solution)/shard_map/ppermute | solution.py:54
  128.4 21.3 %collective-permute-start.9 = (bf16[2,128,1024]{2,1,0:T(8,128)(2,1)S(1)}, bf16[2,128,1024]{2,1,0:T(8,128)(2,1)S(1)}, u32[]{:S(2)}, u32[]{:S(2)}) collective-permute-start(bf16[2,128,1024]{2,1,0:T(8,128)(2,1)S(1)} %fusion.36), channel_id=1, source_target_pairs={{0,4},{2,6},{4,0},{6,2},{8,12},{10,14},{12,8},{14,10},{16,20},{18,... | collective-permute-start | bytes 1572872 | tf_op jit(solution)/shard_map/ppermute | solution.py:54
  129.2 31.7 %collective-permute-start.17 = (bf16[2,128,1024]{2,1,0:T(8,128)(2,1)S(1)}, bf16[2,128,1024]{2,1,0:T(8,128)(2,1)S(1)}, u32[]{:S(2)}, u32[]{:S(2)}) collective-permute-start(bf16[2,128,1024]{2,1,0:T(8,128)(2,1)S(1)} %fusion.35), channel_id=1, source_target_pairs={{0,4},{2,6},{4,0},{6,2},{8,12},{10,14},{12,8},{14,10},{16,20},{18,... | collective-permute-start | bytes 1572872 | tf_op jit(solution)/shard_map/ppermute | solution.py:54
  131.7 39.7 %collective-permute-start.15 = (bf16[2,128,1024]{2,1,0:T(8,128)(2,1)S(1)}, bf16[2,128,1024]{2,1,0:T(8,128)(2,1)S(1)}, u32[]{:S(2)}, u32[]{:S(2)}) collective-permute-start(bf16[2,128,1024]{2,1,0:T(8,128)(2,1)S(1)} %fusion.34), channel_id=1, source_target_pairs={{0,4},{2,6},{4,0},{6,2},{8,12},{10,14},{12,8},{14,10},{16,20},{18,... | collective-permute-start | bytes 1572872 | tf_op jit(solution)/shard_map/ppermute | solution.py:54
  150.5 25.5 %collective-permute-start.12 = (bf16[2,128,1024]{2,1,0:T(8,128)(2,1)S(1)}, bf16[2,128,1024]{2,1,0:T(8,128)(2,1)S(1)}, u32[]{:S(2)}, u32[]{:S(2)}) collective-permute-start(bf16[2,128,1024]{2,1,0:T(8,128)(2,1)S(1)} %fusion.33), channel_id=1, source_target_pairs={{0,8},{2,10},{4,12},{6,14},{8,0},{10,2},{12,4},{14,6},{16,24},{18,... | collective-permute-start | bytes 1572872 | tf_op jit(solution)/shard_map/ppermute | solution.py:54
  171.9 2.2 %copy-start.6 = (bf16[2048,1024]{1,0:T(8,128)(2,1)S(1)}, bf16[2048,1024]{1,0:T(8,128)(2,1)}, u32[]{:S(2)}) copy-start(bf16[2048,1024]{1,0:T(8,128)(2,1)} %shard_map.87) | copy-start | bytes 12582916
  172.3 18.9 %collective-permute-start.18 = (bf16[2,128,1024]{2,1,0:T(8,128)(2,1)S(1)}, bf16[2,128,1024]{2,1,0:T(8,128)(2,1)S(1)}, u32[]{:S(2)}, u32[]{:S(2)}) collective-permute-start(bf16[2,128,1024]{2,1,0:T(8,128)(2,1)S(1)} %fusion.38), channel_id=1, source_target_pairs={{0,8},{2,10},{4,12},{6,14},{8,0},{10,2},{12,4},{14,6},{16,24},{18,... | collective-permute-start | bytes 1572872 | tf_op jit(solution)/shard_map/ppermute | solution.py:54
  174.1 19.6 %copy-start.16 = (f32[768,1024]{1,0:T(8,128)S(1)}, f32[768,1024]{1,0:T(8,128)}, u32[]{:S(2)}) copy-start(f32[768,1024]{1,0:T(8,128)} %fusion.7) | copy-start | bytes 9437188
  174.1 19.6 %copy-start.17 = (f32[768,1024]{1,0:T(8,128)S(1)}, f32[768,1024]{1,0:T(8,128)}, u32[]{:S(2)}) copy-start(f32[768,1024]{1,0:T(8,128)} %fusion.3) | copy-start | bytes 9437188
  175.9 17.8 %copy-start.4 = (bf16[2048,1024]{1,0:T(8,128)(2,1)S(1)}, bf16[2048,1024]{1,0:T(8,128)(2,1)}, u32[]{:S(2)}) copy-start(bf16[2048,1024]{1,0:T(8,128)(2,1)} %shard_map.91) | copy-start | bytes 12582916
  176.1 20.6 %collective-permute-start.13 = (bf16[1,128,1024]{2,1,0:T(8,128)(2,1)S(1)}, bf16[1,128,1024]{2,1,0:T(8,128)(2,1)S(1)}, u32[]{:S(2)}, u32[]{:S(2)}) collective-permute-start(bf16[1,128,1024]{2,1,0:T(8,128)(2,1)S(1)} %dynamic-slice_convert_fusion.2), channel_id=1, source_target_pairs={{0,16},{2,18},{4,20},{6,22},{8,24},{10,26},{12,28},{14,30},{16,0},... | collective-permute-start | bytes 786440 | tf_op jit(solution)/shard_map/ppermute | solution.py:54
  191.4 13.8 %collective-permute-start.19 = (bf16[1,128,1024]{2,1,0:T(8,128)(2,1)S(1)}, bf16[1,128,1024]{2,1,0:T(8,128)(2,1)S(1)}, u32[]{:S(2)}, u32[]{:S(2)}) collective-permute-start(bf16[1,128,1024]{2,1,0:T(8,128)(2,1)S(1)} %dynamic-slice_convert_fusion.1), channel_id=1, source_target_pairs={{0,16},{2,18},{4,20},{6,22},{8,24},{10,26},{12,28},{14,30},{16,0},... | collective-permute-start | bytes 786440 | tf_op jit(solution)/shard_map/ppermute | solution.py:54
